TPU v7x, 32 devices: a whole 2x2x4 slice. The times are simulated.
32 devices in a mesh: wide: 8 (over z, core), narrow: 4 (over y, x).
Axes of the slice: x: 2, y: 2, z: 4, core: 2. Of those that a mesh axis runs over, the one named last changes fastest.
Arguments:
- tridiag_vectors: float32 [128, 131072], P(('wide', 'narrow')), may hold values from -6 to 6
- reflectors: float32 [2, 131072, 256], P(None, 'wide'), may hold values from -0.015625 to 0.015625
- triangles: float32 [2, 256, 256], replicated, as said below
- lower_blocks: float32 [6, 1536, 1536], P(None, 'wide'), may hold values from -0.109375 to 0.109375
- diag_inverses: float32 [4, 1536, 1536], P(None, None, 'wide'), as said below
Outputs:
- transformed: float32 [128, 131072], P('narrow', 'wide')
- solved: float32 [128, 4, 1536], P('narrow', None, 'wide')
Inputs may be any that keep to these rules, and one draw needn't show every extreme that they name: `triangles`: zero below the diagonal, positive on it. `diag_inverses`: zero above the diagonal, positive on it.
All inputs are finite; a program needn't handle non-finite values.
Results may differ from a plain program's by a relative error of at most 0.00019.
Values sent between devices are 32-bit elements; how exact they have to be, the bound alone decides.
A program may use at most 128 MiB of HBM per device.

v0:
```python
import jax
import jax.numpy as jnp
from jax import lax
from jax.sharding import PartitionSpec as P

HIGHEST = lax.Precision.HIGHEST


def reflect(current, vectors, factor, products):
    coeffs = jnp.dot(products, factor.T, precision=HIGHEST)
    return current - jnp.dot(coeffs, vectors.T, precision=HIGHEST)


def add_piece(inverse, segment):
    return jnp.dot(segment, inverse, precision=HIGHEST)


def solve_chain(corner, lower_blocks, diag_inverses):
    local_count, panels, share_cols = corner.shape
    zeroed = jnp.zeros((local_count, share_cols), jnp.float32)
    pending = [zeroed] * panels
    results = [zeroed] * panels
    for source in reversed(range(panels)):
        remain = corner[:, source, :] - pending[source]
        solution = add_piece(
            diag_inverses[source], lax.all_gather(remain, "wide", axis=1, tiled=True)
        )
        results[source] = solution
        if source > 0:
            offset = source * (source - 1) // 2
            blocks = lower_blocks[offset : offset + source]
            partial_terms = jnp.einsum("ks,qsc->kqc", solution, blocks, precision=HIGHEST)
            scattered = lax.psum_scatter(partial_terms, "wide", scatter_dimension=2, tiled=True)
            for target in range(source):
                pending[target] = pending[target] + scattered[:, target, :]
    return jnp.stack(results, axis=1)


def body(tridiag_vectors, reflectors, triangles, lower_blocks, diag_inverses):
    wide_size = lax.axis_size("wide")
    spread = lax.all_to_all(
        tridiag_vectors, ("wide", "narrow"), split_axis=1, concat_axis=0, tiled=True
    )
    current = lax.all_to_all(spread, "narrow", split_axis=0, concat_axis=1, tiled=True)
    for which in (1, 0):
        products = lax.psum(jnp.dot(current, reflectors[which], precision=HIGHEST), "wide")
        current = reflect(current, reflectors[which], triangles[which], products)
    panels, panel_rows, share_cols = diag_inverses.shape
    corner_span = panels * panel_rows
    tail_cols = current[:, current.shape[1] - corner_span :]
    framed = tail_cols.reshape(tail_cols.shape[0], panels, wide_size, share_cols)
    received = lax.all_to_all(framed, "wide", split_axis=2, concat_axis=2, tiled=True)
    corner = received[:, :, wide_size - 1, :]
    solved = solve_chain(corner, lower_blocks, diag_inverses)
    return (current, solved)


def solution(mesh):
    placed = (
        P(("wide", "narrow"), None),
        P(None, "wide", None),
        P(),
        P(None, "wide", None),
        P(None, None, "wide"),
    )
    return jax.shard_map(
        body,
        mesh=mesh,
        in_specs=placed,
        out_specs=(P("narrow", "wide"), P("narrow", None, "wide")),
        check_vma=False,
    )
```

profile of v0, /device:TPU:0, one launch (start us, length us, event | category | flops | bytes accessed | tf_op | source)
XLA Modules:
  0.0 433.0 jit_solution(8765695923981802089)
XLA Ops:
  7.2 0.0 reduce-scatter.10.cloned.1.call-start
  7.2 56.5 %all_to_all.40 = f32[4,32,4096]{2,0,1:T(4,128)} all-to-all(f32[4,32,4096]{2,0,1:T(4,128)} %bitcast.93), channel_id=1, replica_groups=mesh['wide'=8,'narrow'=4] {'wide','narrow'}, dimensions={1} | all-to-all | bytes 4194304 | tf_op jit(solution)/shard_map/all_to_all | solution.py:41
  63.7 2.0 all_to_all.32
  65.6 28.2 %all_to_all.41 = f32[4,32,4096]{2,1,0:T(8,128)S(1)} all-to-all(f32[4,32,4096]{2,1,0:T(8,128)S(1)} %all_to_all.32), channel_id=1, replica_groups=mesh['wide'=8,'narrow'=4] {'narrow'}, dimensions={0} | all-to-all | bytes 4194304 | tf_op jit(solution)/shard_map/all_to_all | solution.py:44
  93.8 0.1 copy.39
  94.0 0.0 copy-start
  94.0 1.3 copy-done
  95.3 0.0 copy-start.2
  95.3 10.7 %fusion.4 = f32[32,256]{1,0:T(8,128)S(1)} fusion(f32[32,16384]{1,0:T(8,128)S(1)} %bitcast.83, f32[2,16384,256]{2,1,0:T(8,128)} %param.6), kind=kOutput, calls=%fused_computation.6 | convolution fusion | flops 1610612736 | bytes 18907136 | tf_op jit(solution)/shard_map/dot_general | solution.py:46
  106.0 26.1 %psum.14 = f32[32,256]{1,0:T(8,128)S(1)} all-reduce(f32[32,256]{1,0:T(8,128)S(1)} %fusion.4), channel_id=1, replica_groups=mesh['wide'=8,'narrow'=4] {'wide'}, use_global_device_ids=true, to_apply=%region_0.0 | all-reduce | flops 8192 | bytes 65536 | tf_op jit(solution)/shard_map/psum | solution.py:46
  132.1 0.0 copy-done.2
  132.1 0.3 fusion.33
  132.5 18.6 %convolution_subtract_fusion.1 = f32[32,16384]{1,0:T(8,128)S(1)} fusion(f32[32,16384]{1,0:T(8,128)} %bitcast.84, f32[32,256]{1,0:T(8,128)S(1)} %fusion.33, f32[2,16384,256]{2,1,0:T(8,128)} %param.6), kind=kOutput, calls=%fused_computation.1 | convolution fusion | flops 1611137024 | bytes 21004288 | tf_op jit(solution)/shard_map/dot_general | solution.py:11
  151.1 10.6 %fusion.1 = f32[32,256]{1,0:T(8,128)S(1)} fusion(f32[32,16384]{1,0:T(8,128)S(1)} %convolution_subtract_fusion.1, f32[2,16384,256]{2,1,0:T(8,128)} %param.6), kind=kOutput, calls=%fused_computation.3 | convolution fusion | flops 1610612736 | bytes 18907136 | tf_op jit(solution)/shard_map/dot_general | solution.py:46
  161.8 26.2 %psum.15 = f32[32,256]{1,0:T(8,128)S(1)} all-reduce(f32[32,256]{1,0:T(8,128)S(1)} %fusion.1), channel_id=1, replica_groups=mesh['wide'=8,'narrow'=4] {'wide'}, use_global_device_ids=true, to_apply=%region_1.0 | all-reduce | flops 8192 | bytes 65536 | tf_op jit(solution)/shard_map/psum | solution.py:46
  187.9 0.3 fusion.31
  188.3 17.3 %convolution_subtract_fusion = f32[32,16384]{1,0:T(8,128)S(1)} fusion(f32[32,16384]{1,0:T(8,128)S(1)} %convolution_subtract_fusion.1, f32[32,256]{1,0:T(8,128)S(1)} %fusion.31, f32[2,16384,256]{2,1,0:T(8,128)} %param.6), kind=kOutput, calls=%fused_computation | convolution fusion | flops 1611137024 | bytes 21004288 | tf_op jit(solution)/shard_map/dot_general | solution.py:11
  205.5 0.0 copy-start.1
  205.5 1.3 copy-done.1
  206.9 0.1 slice.90
  206.9 0.5 reshape.24
  207.4 0.6 copy.22
  208.0 29.0 %all_to_all.42 = f32[32,4,8,192]{3,0,1,2:T(8,128)S(1)} all-to-all(f32[32,4,8,192]{3,0,1,2:T(8,128)S(1)} %copy.22), channel_id=1, replica_groups=mesh['wide'=8,'narrow'=4] {'wide'}, dimensions={2} | all-to-all | bytes 1572864 | tf_op jit(solution)/shard_map/all_to_all | solution.py:52
  237.0 0.1 copy.23
  237.1 15.7 %all-gather = f32[32,1,1536]{0,1,2:T(1,128)S(1)} all-gather(f32[32,1,192]{0,1,2:T(1,128)S(1)} %copy.23), channel_id=2, replica_groups=mesh['wide'=8,'narrow'=4] {'wide'}, dimensions={2}, use_global_device_ids=true | all-gather | bytes 221184 | tf_op jit(solution)/shard_map/all_gather | solution.py:26
  252.9 2.6 fusion.21
  255.5 5.0 %fusion.10 = f32[32,3,1536]{2,0,1:T(8,128)} fusion(f32[6,192,1536]{2,1,0:T(8,128)} %param.8, f32[32,192]{1,0:T(8,128)S(1)} %fusion.21), kind=kOutput, calls=%fused_computation.12 | convolution fusion | flops 339738624 | bytes 4153344 | tf_op jit(solution)/shard_map/ks,qsc->kqc/dot_general | solution.py:32
  260.5 2.6 copy.28
  263.2 2.2 reshape.32
  265.4 0.0 reduce-scatter.10.cloned.1.call-update
  265.4 0.0 reduce-scatter.12.cloned.1.call-start
  265.5 29.5 %reduce-scatter.10.cloned.1.call-done = f32[192,96]{1,0:T(8,128)} async-done(((f32[1536,96]{1,0:T(8,128)}), f32[192,96]{1,0:T(8,128)}) %reduce-scatter.10.cloned.1.call-update) | async-done | bytes 73744
  295.0 1.1 reshape.33
  296.1 0.2 fusion.39
  296.3 0.1 copy.35
  296.4 0.1 copy.24
  296.5 16.0 %all-gather.1 = f32[32,1,1536]{0,1,2:T(1,128)S(1)} all-gather(f32[32,1,192]{0,1,2:T(1,128)S(1)} %copy.24), channel_id=3, replica_groups=mesh['wide'=8,'narrow'=4] {'wide'}, dimensions={2}, use_global_device_ids=true | all-gather | bytes 221184 | tf_op jit(solution)/shard_map/all_gather | solution.py:26
  312.5 2.6 fusion.19
  315.1 3.2 fusion.12
  318.3 0.8 copy.30
  319.1 1.8 reshape.34
  320.9 0.0 reduce-scatter.12.cloned.1.call-update
  320.9 0.0 reduce-scatter.14.cloned.1.call-start
  321.0 0.1 copy.37
  321.0 30.2 %reduce-scatter.12.cloned.1.call-done = f32[192,64]{1,0:T(8,128)} async-done(((f32[1536,64]{1,0:T(8,128)}), f32[192,64]{1,0:T(8,128)}) %reduce-scatter.12.cloned.1.call-update) | async-done | bytes 49168
  351.2 1.0 reshape.35
  352.3 0.2 fusion.40
  352.4 0.1 copy.38
  352.5 0.1 copy.25
  352.6 15.7 %all-gather.2 = f32[32,1,1536]{0,1,2:T(1,128)S(1)} all-gather(f32[32,1,192]{0,1,2:T(1,128)S(1)} %copy.25), channel_id=4, replica_groups=mesh['wide'=8,'narrow'=4] {'wide'}, dimensions={2}, use_global_device_ids=true | all-gather | bytes 221184 | tf_op jit(solution)/shard_map/all_gather | solution.py:26
  368.4 2.6 fusion.17
  371.0 4.8 %convolution_bitcast_fusion = f32[1536,32]{1,0:T(8,128)} fusion(f32[32,192]{1,0:T(8,128)S(1)} %fusion.17, f32[6,192,1536]{2,1,0:T(8,128)} %param.8), kind=kOutput, calls=%fused_computation.14 | convolution fusion | flops 113246208 | bytes 1400832 | tf_op jit(solution)/shard_map/ks,qsc->kqc/dot_general | solution.py:32
  375.8 0.0 reduce-scatter.14.cloned.1.call-update
  375.8 0.1 copy.34
  375.9 0.1 copy.36
  375.9 30.3 %reduce-scatter.14.cloned.1.call-done = f32[192,32]{1,0:T(8,128)} async-done(((f32[1536,32]{1,0:T(8,128)}), f32[192,32]{1,0:T(8,128)}) %reduce-scatter.14.cloned.1.call-update) | async-done | bytes 24592
  406.3 1.0 copy.33
  407.2 0.1 copy.26
  407.3 15.7 %all-gather.3 = f32[32,1,1536]{0,1,2:T(1,128)S(1)} all-gather(f32[32,1,192]{0,1,2:T(1,128)S(1)} %copy.26), channel_id=5, replica_groups=mesh['wide'=8,'narrow'=4] {'wide'}, dimensions={2}, use_global_device_ids=true | all-gather | bytes 221184 | tf_op jit(solution)/shard_map/all_gather | solution.py:26
  423.1 2.6 fusion.28
  425.7 0.7 copy.27
  (6 shorter events, 0.1 us)
Async XLA Ops:
  7.2 287.9 %reduce-scatter.10.cloned.1.call-start = ((), (), s32[]{:S(2)}) async-start(), calls=%async_computation.6 | async-start | bytes 884736
  94.0 1.3 copy-start
  95.3 36.8 %copy-start.2 = (f32[2,256,256]{2,1,0:T(8,128)S(1)}, f32[2,256,256]{2,1,0:T(8,128)}, u32[]{:S(2)}) copy-start(f32[2,256,256]{2,1,0:T(8,128)} %param.7) | copy-start | bytes 1572868
  205.5 1.3 copy-start.1
  265.4 85.8 %reduce-scatter.12.cloned.1.call-start = ((), (), s32[]{:S(2)}) async-start(), calls=%async_computation.7 | async-start | bytes 884736
  320.9 85.4 %reduce-scatter.14.cloned.1.call-start = ((), (), s32[]{:S(2)}) async-start(), calls=%async_computation.8 | async-start | bytes 884736
Sparse Core Ops, SparseCore 0:
  265.6 29.4 reduce-scatter.9
  321.0 30.1 reduce-scatter.11
  375.9 30.2 reduce-scatter.13
where the time goes:
time: 434 us; the launch traced here: 433 us
  blocking collectives  229 us (53%)
  waiting for transfers between devices  90.1 us (21%)
  matrix products  81.5 us (19%)
  local copies, waits for them, and re-layouts  18.2 us (4%)
  between operations  14 us (3%)
    unnamed x6, waiting for transfers between devices  90.1 us
    all_gather x4, blocking collectives, solve_chain(): lax.all_gather(remain, 'wide', axis=1, tiled=True)  63.2 us
    all_to_all x1, blocking collectives, body(): lax.all_to_all(tridiag_vectors, ('wide', 'narrow'), split_axis=1, concat_...  56.5 us
    psum x2, blocking collectives, body(): lax.psum(jnp.dot(current, reflectors[which], precision=HIGHEST), 'wide')  52.3 us
    dot_general x2, matrix products, reflect(): return current - jnp.dot(coeffs, vectors.T, precision=HIGHEST)  35.9 us
    all_to_all x1, blocking collectives, body(): lax.all_to_all(framed, 'wide', split_axis=2, concat_axis=2, tiled=True)  29 us
    all_to_all x1, blocking collectives, body(): lax.all_to_all(spread, 'narrow', split_axis=0, concat_axis=1, tiled=True)  28.2 us
    dot_general x2, matrix products, body(): jnp.dot(current, reflectors[which], precision=HIGHEST)  21.3 us
  transfers between devices with their start and end apart: 3, of which 3 were waited for; matrix products, arithmetic and copies ran while one was open for 0% of the time, Pallas kernels for 0%

commit v1 on v0

--- a/solution.py
+++ b/solution.py
@@ -43,7 +43,9 @@
     )
     current = lax.all_to_all(spread, "narrow", split_axis=0, concat_axis=1, tiled=True)
     for which in (1, 0):
-        products = lax.psum(jnp.dot(current, reflectors[which], precision=HIGHEST), "wide")
+        products = jnp.sum(
+            lax.all_gather(jnp.dot(current, reflectors[which], precision=HIGHEST), "wide"), axis=0
+        )
         current = reflect(current, reflectors[which], triangles[which], products)
     panels, panel_rows, share_cols = diag_inverses.shape
     corner_span = panels * panel_rows

time: 434 us -> 410 us (0.945)
  blocking collectives: 229 us -> 206 us
    psum x2 -> x0, blocking collectives: 52.3 us -> none  [body(): lax.psum(jnp.dot(current, reflectors[which], precision=HIGHEST), 'wide')]
    all_gather x0 -> x2, blocking collectives: none -> 28.8 us  [body(): lax.all_gather(jnp.dot(current, reflectors[which], precision=HIGHEST), 'w...]
where the time goes in v1:
time: 410 us
  blocking collectives  206 us (50%)
  waiting for transfers between devices  89.9 us (22%)
  matrix products  82.2 us (20%)
  local copies, waits for them, and re-layouts  16.9 us (4%)
  between operations  14 us (3%)
    unnamed x6, waiting for transfers between devices  89.9 us
    all_gather x4, blocking collectives, solve_chain(): lax.all_gather(remain, 'wide', axis=1, tiled=True)  63.2 us
    all_to_all x1, blocking collectives, body(): lax.all_to_all(tridiag_vectors, ('wide', 'narrow'), split_axis=1, concat_...  56.5 us
    dot_general x2, matrix products, reflect(): return current - jnp.dot(coeffs, vectors.T, precision=HIGHEST)  35.9 us
    all_to_all x1, blocking collectives, body(): lax.all_to_all(framed, 'wide', split_axis=2, concat_axis=2, tiled=True)  29.7 us
    all_gather x2, blocking collectives, body(): lax.all_gather(jnp.dot(current, reflectors[which], precision=HIGHEST), 'w...  28.8 us
    all_to_all x1, blocking collectives, body(): lax.all_to_all(spread, 'narrow', split_axis=0, concat_axis=1, tiled=True)  28.2 us
    dot_general x2, matrix products, body(): jnp.dot(current, reflectors[which], precision=HIGHEST)  22.1 us
  transfers between devices with their start and end apart: 3, of which 3 were waited for; matrix products, arithmetic and copies ran while one was open for 0% of the time, Pallas kernels for 0%

profile of v1, /device:TPU:0, one launch (start us, length us, event | category | flops | bytes accessed | tf_op | source)
XLA Modules:
  0.0 409.5 jit_solution(6941237816644006626)
XLA Ops:
  7.2 0.0 reduce-scatter.10.cloned.1.call-start
  7.2 56.5 %all_to_all.40 = f32[4,32,4096]{2,0,1:T(4,128)} all-to-all(f32[4,32,4096]{2,0,1:T(4,128)} %bitcast.95), channel_id=1, replica_groups=mesh['wide'=8,'narrow'=4] {'wide','narrow'}, dimensions={1} | all-to-all | bytes 4194304 | tf_op jit(solution)/shard_map/all_to_all | solution.py:41
  63.7 2.0 all_to_all.32
  65.6 28.2 %all_to_all.41 = f32[4,32,4096]{2,1,0:T(8,128)S(1)} all-to-all(f32[4,32,4096]{2,1,0:T(8,128)S(1)} %all_to_all.32), channel_id=1, replica_groups=mesh['wide'=8,'narrow'=4] {'narrow'}, dimensions={0} | all-to-all | bytes 4194304 | tf_op jit(solution)/shard_map/all_to_all | solution.py:44
  93.8 0.1 copy.39
  94.0 0.0 copy-start
  94.0 0.0 copy-start.2
  94.0 11.4 %fusion.4 = f32[32,256]{1,0:T(8,128)S(1)} fusion(f32[32,16384]{1,0:T(8,128)S(1)} %bitcast.85, f32[2,16384,256]{2,1,0:T(8,128)} %param.6), kind=kOutput, calls=%fused_computation.6 | convolution fusion | flops 1610612736 | bytes 18907136 | tf_op jit(solution)/shard_map/dot_general | solution.py:47
  105.4 0.0 copy-done
  105.4 14.4 %all-gather = f32[256,256]{1,0:T(8,128)S(1)} all-gather(f32[32,256]{1,0:T(8,128)S(1)} %fusion.4), channel_id=2, replica_groups=mesh['wide'=8,'narrow'=4] {'wide'}, dimensions={0}, use_global_device_ids=true | all-gather | bytes 294912 | tf_op jit(solution)/shard_map/all_gather | solution.py:47
  119.8 0.0 copy-done.2
  119.8 0.3 fusion.33
  120.2 18.6 %convolution_subtract_fusion.1 = f32[32,16384]{1,0:T(8,128)S(1)} fusion(f32[32,16384]{1,0:T(8,128)} %bitcast.86, f32[32,256]{1,0:T(8,128)S(1)} %fusion.33, f32[2,16384,256]{2,1,0:T(8,128)} %param.6), kind=kOutput, calls=%fused_computation.1 | convolution fusion | flops 1611137024 | bytes 21004288 | tf_op jit(solution)/shard_map/dot_general | solution.py:11
  138.8 10.7 %fusion.1 = f32[32,256]{1,0:T(8,128)S(1)} fusion(f32[32,16384]{1,0:T(8,128)S(1)} %convolution_subtract_fusion.1, f32[2,16384,256]{2,1,0:T(8,128)} %param.6), kind=kOutput, calls=%fused_computation.3 | convolution fusion | flops 1610612736 | bytes 18907136 | tf_op jit(solution)/shard_map/dot_general | solution.py:47
  149.5 14.4 %all-gather.1 = f32[256,256]{1,0:T(8,128)S(1)} all-gather(f32[32,256]{1,0:T(8,128)S(1)} %fusion.1), channel_id=3, replica_groups=mesh['wide'=8,'narrow'=4] {'wide'}, dimensions={0}, use_global_device_ids=true | all-gather | bytes 294912 | tf_op jit(solution)/shard_map/all_gather | solution.py:47
  163.9 0.3 fusion.31
  164.2 17.3 %convolution_subtract_fusion = f32[32,16384]{1,0:T(8,128)S(1)} fusion(f32[32,16384]{1,0:T(8,128)S(1)} %convolution_subtract_fusion.1, f32[32,256]{1,0:T(8,128)S(1)} %fusion.31, f32[2,16384,256]{2,1,0:T(8,128)} %param.6), kind=kOutput, calls=%fused_computation | convolution fusion | flops 1611137024 | bytes 21004288 | tf_op jit(solution)/shard_map/dot_general | solution.py:11
  181.5 0.0 copy-start.1
  181.5 1.3 copy-done.1
  182.8 0.1 slice.90
  182.9 0.5 reshape.24
  183.4 0.6 copy.22
  184.0 29.7 %all_to_all.42 = f32[32,4,8,192]{3,0,1,2:T(8,128)S(1)} all-to-all(f32[32,4,8,192]{3,0,1,2:T(8,128)S(1)} %copy.22), channel_id=1, replica_groups=mesh['wide'=8,'narrow'=4] {'wide'}, dimensions={2} | all-to-all | bytes 1572864 | tf_op jit(solution)/shard_map/all_to_all | solution.py:54
  213.7 0.1 copy.23
  213.8 15.7 %all-gather.2 = f32[32,1,1536]{0,1,2:T(1,128)S(1)} all-gather(f32[32,1,192]{0,1,2:T(1,128)S(1)} %copy.23), channel_id=4, replica_groups=mesh['wide'=8,'narrow'=4] {'wide'}, dimensions={2}, use_global_device_ids=true | all-gather | bytes 221184 | tf_op jit(solution)/shard_map/all_gather | solution.py:26
  229.6 2.6 fusion.21
  232.2 5.0 %fusion.10 = f32[32,3,1536]{2,0,1:T(8,128)} fusion(f32[6,192,1536]{2,1,0:T(8,128)} %param.8, f32[32,192]{1,0:T(8,128)S(1)} %fusion.21), kind=kOutput, calls=%fused_computation.12 | convolution fusion | flops 339738624 | bytes 4153344 | tf_op jit(solution)/shard_map/ks,qsc->kqc/dot_general | solution.py:32
  237.3 2.6 copy.28
  239.9 2.2 reshape.34
  242.1 0.0 reduce-scatter.10.cloned.1.call-update
  242.1 0.0 reduce-scatter.12.cloned.1.call-start
  242.2 29.2 %reduce-scatter.10.cloned.1.call-done = f32[192,96]{1,0:T(8,128)} async-done(((f32[1536,96]{1,0:T(8,128)}), f32[192,96]{1,0:T(8,128)}) %reduce-scatter.10.cloned.1.call-update) | async-done | bytes 73744
  271.4 1.1 reshape.35
  272.5 0.2 fusion.39
  272.7 0.1 copy.35
  272.8 0.1 copy.24
  272.9 16.0 %all-gather.3 = f32[32,1,1536]{0,1,2:T(1,128)S(1)} all-gather(f32[32,1,192]{0,1,2:T(1,128)S(1)} %copy.24), channel_id=5, replica_groups=mesh['wide'=8,'narrow'=4] {'wide'}, dimensions={2}, use_global_device_ids=true | all-gather | bytes 221184 | tf_op jit(solution)/shard_map/all_gather | solution.py:26
  288.9 2.6 fusion.19
  291.5 3.2 fusion.12
  294.7 0.8 copy.30
  295.5 1.8 reshape.36
  297.3 0.0 reduce-scatter.12.cloned.1.call-update
  297.3 0.0 reduce-scatter.14.cloned.1.call-start
  297.4 0.1 copy.37
  297.4 30.3 %reduce-scatter.12.cloned.1.call-done = f32[192,64]{1,0:T(8,128)} async-done(((f32[1536,64]{1,0:T(8,128)}), f32[192,64]{1,0:T(8,128)}) %reduce-scatter.12.cloned.1.call-update) | async-done | bytes 49168
  327.8 1.0 reshape.37
  328.8 0.2 fusion.40
  329.0 0.1 copy.38
  329.1 0.1 copy.25
  329.2 15.7 %all-gather.4 = f32[32,1,1536]{0,1,2:T(1,128)S(1)} all-gather(f32[32,1,192]{0,1,2:T(1,128)S(1)} %copy.25), channel_id=6, replica_groups=mesh['wide'=8,'narrow'=4] {'wide'}, dimensions={2}, use_global_device_ids=true | all-gather | bytes 221184 | tf_op jit(solution)/shard_map/all_gather | solution.py:26
  344.9 2.6 fusion.17
  347.5 4.8 %convolution_bitcast_fusion = f32[1536,32]{1,0:T(8,128)} fusion(f32[32,192]{1,0:T(8,128)S(1)} %fusion.17, f32[6,192,1536]{2,1,0:T(8,128)} %param.8), kind=kOutput, calls=%fused_computation.14 | convolution fusion | flops 113246208 | bytes 1400832 | tf_op jit(solution)/shard_map/ks,qsc->kqc/dot_general | solution.py:32
  352.3 0.0 reduce-scatter.14.cloned.1.call-update
  352.3 0.1 copy.34
  352.4 0.1 copy.36
  352.5 30.3 %reduce-scatter.14.cloned.1.call-done = f32[192,32]{1,0:T(8,128)} async-done(((f32[1536,32]{1,0:T(8,128)}), f32[192,32]{1,0:T(8,128)}) %reduce-scatter.14.cloned.1.call-update) | async-done | bytes 24592
  382.8 1.0 copy.33
  383.8 0.1 copy.26
  383.9 15.7 %all-gather.5 = f32[32,1,1536]{0,1,2:T(1,128)S(1)} all-gather(f32[32,1,192]{0,1,2:T(1,128)S(1)} %copy.26), channel_id=7, replica_groups=mesh['wide'=8,'narrow'=4] {'wide'}, dimensions={2}, use_global_device_ids=true | all-gather | bytes 221184 | tf_op jit(solution)/shard_map/all_gather | solution.py:26
  399.6 2.6 fusion.28
  402.3 0.7 copy.27
  (8 shorter events, 0.1 us)
Async XLA Ops:
  7.2 264.3 %reduce-scatter.10.cloned.1.call-start = ((), (), s32[]{:S(2)}) async-start(), calls=%async_computation.6 | async-start | bytes 884736
  94.0 11.5 %copy-start = (f32[4,4,8,4096]{3,2,0,1:T(8,128)}, f32[4,4,8,4096]{3,2,0,1:T(8,128)S(1)}, u32[]{:S(2)}) copy-start(f32[4,4,8,4096]{3,2,0,1:T(8,128)S(1)} %copy.39) | copy-start | bytes 6291460
  94.0 25.8 %copy-start.2 = (f32[2,256,256]{2,1,0:T(8,128)S(1)}, f32[2,256,256]{2,1,0:T(8,128)}, u32[]{:S(2)}) copy-start(f32[2,256,256]{2,1,0:T(8,128)} %param.7) | copy-start | bytes 1572868
  181.5 1.3 copy-start.1
  242.1 85.6 %reduce-scatter.12.cloned.1.call-start = ((), (), s32[]{:S(2)}) async-start(), calls=%async_computation.7 | async-start | bytes 884736
  297.3 85.5 %reduce-scatter.14.cloned.1.call-start = ((), (), s32[]{:S(2)}) async-start(), calls=%async_computation.8 | async-start | bytes 884736
Sparse Core Ops, SparseCore 0:
  242.3 29.1 reduce-scatter.9
  297.4 30.2 reduce-scatter.11
  352.5 30.2 reduce-scatter.13
